TPU v7x, 128 devices: a whole 4x4x4 slice. The times are simulated.
128 devices in a mesh: sub: 4 (over x_hi, core), brick: 32 (over x_lo, z, y).
Axes of the slice: x: 4 (x_hi: 2, x_lo: 2; x = x_hi * 2 + x_lo), y: 4, z: 4, core: 2. Of those that a mesh axis runs over, the one named last changes fastest.
Arguments:
- increments: float32 [8, 128, 256, 512], P('sub', None, 'brick'), may hold values from -6 to 6
- courant_x: float32 [8, 128, 256, 512], P('sub', None, 'brick'), may hold values from -0.5 to 0.5
- courant_y: float32 [8, 128, 256, 512], P('sub', None, 'brick'), may hold values from -0.5 to 0.5
- spectrum: float32 [256, 512], replicated, may hold values from 0.05 to 2
- vertical: float32 [128, 128], replicated, may hold values from -0.5 to 0.5
Outputs:
- covaried: float32 [8, 128, 256, 512], P('sub', None, 'brick')
All inputs are finite; a program needn't handle non-finite values.
Results may differ from a plain program's by a relative error of at most 0.00007.
Values sent between devices are 32-bit elements; how exact they have to be, the bound alone decides.
A program may use at most 192 MiB of HBM per device.

v0:
```python
import jax
import jax.numpy as jnp
from jax import lax
from jax.sharding import PartitionSpec as P

STEPS = 4


diffusion = 0.2


def extended_2(value, sides, width):
    for axis, dim in sides:
        count, length = (lax.axis_size(axis), value.shape[dim])
        up = [(i, (i + 1) % count) for i in range(count - 1)]
        down = [(j, i) for i, j in up]
        last = lax.slice_in_dim(value, length - width, length, axis=dim)
        initial = lax.slice_in_dim(value, 0, width, axis=dim)
        before = lax.ppermute(last, axis, up)
        after = lax.ppermute(initial, axis, down)
        value = jnp.concatenate([before, value, after], axis=dim)
    return value


def shifted(value, axis, by):
    count = lax.axis_size(axis)
    pairs = [(i, i + by) for i in range(count) if 0 <= i + by < count]
    return lax.ppermute(value, axis, pairs)


def exchange_in_groups(value, axis, split_dim, concat_dim, work, item_dim, out_dim):

    def moved(group):
        return lax.all_to_all(group, axis, split_axis=split_dim, concat_axis=concat_dim, tiled=True)

    items = jax.tree.leaves(value)[0].shape[item_dim]
    ends = [items * k // 2 for k in range(2 + 1)] if items % 2 == 0 else [0, items]
    groups = [
        jax.tree.map(lambda a: lax.slice_in_dim(a, low, high, axis=item_dim), value)
        for low, high in zip(ends, ends[1:])
    ]
    arrived = [moved(group) for group in groups]
    made = [work(group) for group in arrived]
    return jax.tree.map(lambda *parts: jnp.concatenate(parts, axis=out_dim), *made)


def dct_table(count):
    freq = jnp.arange(count, dtype=jnp.float32)[:, None]
    cells = jnp.arange(count, dtype=jnp.float32)[None, :]
    table = jnp.cos(jnp.pi * (cells + 0.5) * freq / count) * jnp.sqrt(jnp.float32(2.0) / count)
    first = jnp.where(jnp.arange(count)[:, None] == 0, jnp.sqrt(jnp.float32(0.5)), jnp.float32(1.0))
    return table * first


def advance(extended, courant_x, courant_y):
    center = extended[..., 1:-1, :]
    north = extended[..., 2:, :]
    south = extended[..., :-2, :]
    widths = [(0, 0)] * (center.ndim - 1) + [(1, 1)]
    padded = jnp.pad(center, widths)
    east = padded[..., 2:]
    west = padded[..., :-2]
    return (
        center
        - 0.5 * courant_x * (north - south)
        - 0.5 * courant_y * (east - west)
        + diffusion * (north + south + east + west - 4.0 * center)
    )


def on_device(increments, courant_x, courant_y, spectrum, vertical):
    high = lax.Precision.HIGHEST
    rows = increments.shape[2]
    total_rows = rows * lax.axis_size("brick")
    state = increments
    for number in range(STEPS):
        extended = extended_2(state, (("brick", 2),), 1)
        state = advance(extended, courant_x, courant_y)
    prior = shifted(state[-1], "sub", 1)
    previous = jnp.concatenate([prior[None], state[:-1]], axis=0)
    jumps = increments - previous
    row_table = dct_table(total_rows)
    col_table = dct_table(increments.shape[3])

    def planes(block):
        forward = jnp.einsum("kx,slxy->slky", row_table, block, precision=high)
        forward = jnp.einsum("slky,jy->slkj", forward, col_table, precision=high)
        scaled = forward * spectrum
        back = jnp.einsum("slkj,jy->slky", scaled, col_table, precision=high)
        back = jnp.einsum("kx,slky->slxy", row_table, back, precision=high)
        return lax.all_to_all(back, "brick", split_axis=2, concat_axis=1, tiled=True)

    horizontal = exchange_in_groups(jumps, "brick", 1, 2, planes, 0, 0)
    return jnp.einsum("ml,slxy->smxy", vertical, horizontal, precision=high)


def solution(mesh):
    in_specs = (
        P("sub", None, "brick", None),
        P("sub", None, "brick", None),
        P("sub", None, "brick", None),
        P(),
        P(),
    )
    out_specs = P("sub", None, "brick", None)
    return jax.shard_map(
        on_device, mesh=mesh, in_specs=in_specs, out_specs=out_specs, check_vma=False
    )
```

profile of v0, /device:TPU:3, one launch (start us, length us, event | category | flops | bytes accessed | tf_op | source)
XLA Modules:
  0.0 303.7 jit_solution(15633212968675816419)
XLA Ops:
  0.0 0.0 copy-start
  0.0 4.5 %fusion.70 = (f32[2,128,1,512]{3,2,0,1:T(1,128)S(1)}, f32[2,128,1,512]{3,2,0,1:T(1,128)S(1)}) fusion(f32[2,128,8,512]{3,2,1,0:T(8,128)} %param.5), kind=kLoop, calls=%fused_computation.103 | loop fusion | bytes 2097152 | tf_op jit(solution)/shard_map/slice | solution.py:17
  4.6 8.1 %collective-permute-start = (f32[2,128,1,512]{3,2,0,1:T(1,128)S(1)}, f32[2,128,1,512]{3,2,0,1:T(1,128)S(1)}, u32[]{:S(2)}, u32[]{:S(2)}) collective-permute-start(f32[2,128,1,512]{3,2,0,1:T(1,128)S(1)} %get-tuple-element.16), channel_id=1, source_target_pairs={{1,0},{2,1},{3,2},{4,3},{5,4},{6,5},{7,6},{8,7},{9,8},{10,9},{11,1... | collective-permute-start | bytes 1572872 | tf_op jit(solution)/shard_map/ppermute | solution.py:20
  12.6 0.0 copy-start.1
  12.7 0.0 copy-start.2
  12.7 2.3 collective-permute-start.1
  15.0 2.7 copy.45
  17.7 5.5 %collective-permute-done = f32[2,128,1,512]{3,2,0,1:T(1,128)S(1)} collective-permute-done((f32[2,128,1,512]{3,2,0,1:T(1,128)S(1)}, f32[2,128,1,512]{3,2,0,1:T(1,128)S(1)}, u32[]{:S(2)}, u32[]{:S(2)}) %collective-permute-start) | collective-permute-done | bytes 524320 | tf_op jit(solution)/shard_map/ppermute | solution.py:20
  23.2 8.3 %collective-permute-done.1 = f32[2,128,1,512]{3,2,0,1:T(1,128)S(1)} collective-permute-done((f32[2,128,1,512]{3,2,0,1:T(1,128)S(1)}, f32[2,128,1,512]{3,2,0,1:T(1,128)S(1)}, u32[]{:S(2)}, u32[]{:S(2)}) %collective-permute-start.1) | collective-permute-done | bytes 524320 | tf_op jit(solution)/shard_map/ppermute | solution.py:19
  31.6 0.0 copy-done.1
  31.6 0.0 copy-done.2
  31.6 4.4 %multiply_add_fusion.3 = f32[2,128,8,512]{3,2,0,1:T(8,128)S(1)} fusion(f32[2,128,8,512]{3,2,0,1:T(8,128)S(1)} %copy.45, f32[2,128,1,512]{3,2,0,1:T(1,128)S(1)} %collective-permute-done, f32[2,128,1,512]{3,2,0,1:T(1,128)S(1)} %collective-permute-done.1, f32[2,128,8,512]{3,2,1,0:T(8,128)S(1)} %copy-done.1, f32[2,128,8,512]{3,2,1,0:T(8,128)S(1)} %copy-done.2), kind=kLoop, calls=%fused_computation.26 | loop fusion | flops 17825792 | bytes 17825792 | tf_op jit(solution)/shard_map/add | solution.py:64
  36.0 0.7 fusion.69
  36.7 1.9 collective-permute-start.2
  38.6 3.4 %collective-permute-start.3 = (f32[2,128,1,512]{3,2,0,1:T(1,128)S(1)}, f32[2,128,1,512]{3,2,0,1:T(1,128)S(1)}, u32[]{:S(2)}, u32[]{:S(2)}) collective-permute-start(f32[2,128,1,512]{3,2,0,1:T(1,128)S(1)} %get-tuple-element.13), channel_id=1, source_target_pairs={{0,1},{1,2},{2,3},{3,4},{4,5},{5,6},{6,7},{7,8},{8,9},{9,10},{10,1... | collective-permute-start | bytes 1572872 | tf_op jit(solution)/shard_map/ppermute | solution.py:19
  42.0 8.3 %collective-permute-done.2 = f32[2,128,1,512]{3,2,0,1:T(1,128)S(1)} collective-permute-done((f32[2,128,1,512]{3,2,0,1:T(1,128)S(1)}, f32[2,128,1,512]{3,2,0,1:T(1,128)S(1)}, u32[]{:S(2)}, u32[]{:S(2)}) %collective-permute-start.2) | collective-permute-done | bytes 524320 | tf_op jit(solution)/shard_map/ppermute | solution.py:20
  50.2 6.1 %collective-permute-done.3 = f32[2,128,1,512]{3,2,0,1:T(1,128)S(1)} collective-permute-done((f32[2,128,1,512]{3,2,0,1:T(1,128)S(1)}, f32[2,128,1,512]{3,2,0,1:T(1,128)S(1)}, u32[]{:S(2)}, u32[]{:S(2)}) %collective-permute-start.3) | collective-permute-done | bytes 524320 | tf_op jit(solution)/shard_map/ppermute | solution.py:19
  56.4 4.4 %multiply_add_fusion.2 = f32[2,128,8,512]{3,2,0,1:T(8,128)S(1)} fusion(f32[2,128,8,512]{3,2,0,1:T(8,128)S(1)} %multiply_add_fusion.3, f32[2,128,1,512]{3,2,0,1:T(1,128)S(1)} %collective-permute-done.2, f32[2,128,1,512]{3,2,0,1:T(1,128)S(1)} %collective-permute-done.3, f32[2,128,8,512]{3,2,1,0:T(8,128)S(1)} %copy-done.1, f32[2,128,8,512]{3,2,1,0:T(8,128)S(1)} %copy-done.2), kind=kLoop, calls=%fused_computation.25 | loop fusion | flops 17825792 | bytes 17825792 | tf_op jit(solution)/shard_map/add | solution.py:64
  60.8 0.7 fusion.68
  61.4 1.9 collective-permute-start.4
  63.4 3.4 %collective-permute-start.5 = (f32[2,128,1,512]{3,2,0,1:T(1,128)S(1)}, f32[2,128,1,512]{3,2,0,1:T(1,128)S(1)}, u32[]{:S(2)}, u32[]{:S(2)}) collective-permute-start(f32[2,128,1,512]{3,2,0,1:T(1,128)S(1)} %get-tuple-element.11), channel_id=1, source_target_pairs={{0,1},{1,2},{2,3},{3,4},{4,5},{5,6},{6,7},{7,8},{8,9},{9,10},{10,1... | collective-permute-start | bytes 1572872 | tf_op jit(solution)/shard_map/ppermute | solution.py:19
  66.7 7.4 %collective-permute-done.4 = f32[2,128,1,512]{3,2,0,1:T(1,128)S(1)} collective-permute-done((f32[2,128,1,512]{3,2,0,1:T(1,128)S(1)}, f32[2,128,1,512]{3,2,0,1:T(1,128)S(1)}, u32[]{:S(2)}, u32[]{:S(2)}) %collective-permute-start.4) | collective-permute-done | bytes 524320 | tf_op jit(solution)/shard_map/ppermute | solution.py:20
  74.2 6.1 %collective-permute-done.5 = f32[2,128,1,512]{3,2,0,1:T(1,128)S(1)} collective-permute-done((f32[2,128,1,512]{3,2,0,1:T(1,128)S(1)}, f32[2,128,1,512]{3,2,0,1:T(1,128)S(1)}, u32[]{:S(2)}, u32[]{:S(2)}) %collective-permute-start.5) | collective-permute-done | bytes 524320 | tf_op jit(solution)/shard_map/ppermute | solution.py:19
  80.3 4.4 %multiply_add_fusion.1 = f32[2,128,8,512]{3,2,0,1:T(8,128)S(1)} fusion(f32[2,128,8,512]{3,2,0,1:T(8,128)S(1)} %multiply_add_fusion.2, f32[2,128,1,512]{3,2,0,1:T(1,128)S(1)} %collective-permute-done.4, f32[2,128,1,512]{3,2,0,1:T(1,128)S(1)} %collective-permute-done.5, f32[2,128,8,512]{3,2,1,0:T(8,128)S(1)} %copy-done.1, f32[2,128,8,512]{3,2,1,0:T(8,128)S(1)} %copy-done.2), kind=kLoop, calls=%fused_computation.24 | loop fusion | flops 17825792 | bytes 17825792 | tf_op jit(solution)/shard_map/add | solution.py:64
  84.7 0.7 fusion.67
  85.4 1.9 collective-permute-start.6
  87.3 3.4 %collective-permute-start.7 = (f32[2,128,1,512]{3,2,0,1:T(1,128)S(1)}, f32[2,128,1,512]{3,2,0,1:T(1,128)S(1)}, u32[]{:S(2)}, u32[]{:S(2)}) collective-permute-start(f32[2,128,1,512]{3,2,0,1:T(1,128)S(1)} %get-tuple-element.9), channel_id=1, source_target_pairs={{0,1},{1,2},{2,3},{3,4},{4,5},{5,6},{6,7},{7,8},{8,9},{9,10},{10,1... | collective-permute-start | bytes 1572872 | tf_op jit(solution)/shard_map/ppermute | solution.py:19
  90.7 6.6 %collective-permute-done.6 = f32[2,128,1,512]{3,2,0,1:T(1,128)S(1)} collective-permute-done((f32[2,128,1,512]{3,2,0,1:T(1,128)S(1)}, f32[2,128,1,512]{3,2,0,1:T(1,128)S(1)}, u32[]{:S(2)}, u32[]{:S(2)}) %collective-permute-start.6) | collective-permute-done | bytes 524320 | tf_op jit(solution)/shard_map/ppermute | solution.py:20
  97.2 6.1 %collective-permute-done.7 = f32[2,128,1,512]{3,2,0,1:T(1,128)S(1)} collective-permute-done((f32[2,128,1,512]{3,2,0,1:T(1,128)S(1)}, f32[2,128,1,512]{3,2,0,1:T(1,128)S(1)}, u32[]{:S(2)}, u32[]{:S(2)}) %collective-permute-start.7) | collective-permute-done | bytes 524320 | tf_op jit(solution)/shard_map/ppermute | solution.py:19
  103.4 4.4 %multiply_add_fusion = f32[2,128,8,512]{3,2,0,1:T(8,128)S(1)} fusion(f32[2,128,8,512]{3,2,0,1:T(8,128)S(1)} %multiply_add_fusion.1, f32[2,128,1,512]{3,2,0,1:T(1,128)S(1)} %collective-permute-done.6, f32[2,128,1,512]{3,2,0,1:T(1,128)S(1)} %collective-permute-done.7, f32[2,128,8,512]{3,2,1,0:T(8,128)S(1)} %copy-done.1, f32[2,128,8,512]{3,2,1,0:T(8,128)S(1)} %copy-done.2), kind=kLoop, calls=%fused_computation.23 | loop fusion | flops 17825792 | bytes 17825792 | tf_op jit(solution)/shard_map/add | solution.py:64
  107.8 0.0 copy-start.3
  107.8 0.5 slice_bitcast_fusion
  108.3 8.7 %collective-permute-start.8 = (f32[128,8,512]{2,1,0:T(8,128)S(1)}, f32[128,8,512]{2,1,0:T(8,128)S(1)}, u32[]{:S(2)}, u32[]{:S(2)}) collective-permute-start(f32[128,8,512]{2,1,0:T(8,128)S(1)} %get-tuple-element.7), channel_id=1, source_target_pairs={{0,32},{32,64},{64,96},{1,33},{33,65},{65,97},{2,34},{34,66},{66,9... | collective-permute-start | bytes 6291464 | tf_op jit(solution)/shard_map/ppermute | solution.py:28
  117.1 33.9 %collective-permute-done.8 = f32[128,8,512]{2,1,0:T(8,128)S(1)} collective-permute-done((f32[128,8,512]{2,1,0:T(8,128)S(1)}, f32[128,8,512]{2,1,0:T(8,128)S(1)}, u32[]{:S(2)}, u32[]{:S(2)}) %collective-permute-start.8) | collective-permute-done | bytes 2097184 | tf_op jit(solution)/shard_map/ppermute | solution.py:28
  151.0 1.0 maximum_subtract_fusion
  152.0 1.8 fusion.66
  153.8 30.8 %all_to_all.66 = f32[1,128,8,512]{3,2,0,1:T(8,128)} all-to-all(f32[1,128,8,512]{3,2,0,1:T(8,128)S(1)} %get-tuple-element.5), channel_id=1, replica_groups=mesh['sub'=4,'brick'=32] {'brick'}, dimensions={1} | all-to-all | bytes 4194304 | tf_op jit(solution)/shard_map/all_to_all | solution.py:34
  184.5 4.9 %all-to-all-start.2 = ((f32[1,128,8,512]{3,2,0,1:T(8,128)}), f32[1,128,8,512]{3,2,0,1:T(8,128)S(1)}, u32[]{:S(2)}, u32[]{:S(2)}) async-start(f32[1,128,8,512]{3,2,0,1:T(8,128)} %get-tuple-element.6), calls=%async_computation.2 | async-start | bytes 4194304 | tf_op jit(solution)/shard_map/all_to_all | solution.py:34
  189.5 0.0 copy-start.4
  189.5 6.1 %fusion.13 = f32[4,512,256]{2,1,0:T(8,128)S(1)} fusion(f32[1,4,32,8,512]{4,3,1,2,0:T(8,128)} %bitcast.79, f32[256]{0:T(256)S(1)} %get-tuple-element.17, f32[256]{0:T(256)S(1)} %get-tuple-element.18), kind=kOutput, calls=%fused_computation.35 | convolution fusion | flops 1610809344 | bytes 4196352 | tf_op jit(solution)/shard_map/kx,slxy->slky/dot_general | solution.py:86
  195.6 19.0 %fusion.9 = f32[4,256,512]{2,1,0:T(8,128)S(1)} fusion(f32[4,512,256]{2,1,0:T(8,128)S(1)} %fusion.13, f32[512]{0:T(512)S(1)} %get-tuple-element.19, f32[512]{0:T(512)S(1)} %get-tuple-element.20), kind=kOutput, calls=%fused_computation.31 | convolution fusion | flops 3222011904 | bytes 4198400 | tf_op jit(solution)/shard_map/slky,jy->slkj/dot_general | solution.py:87
  214.5 0.0 copy-done.4
  214.5 7.2 %fusion.19 = f32[4,256,512]{1,2,0:T(8,128)S(1)} fusion(f32[4,256,512]{2,1,0:T(8,128)S(1)} %fusion.9, f32[256,512]{1,0:T(8,128)S(1)} %copy-done.4, f32[512]{0:T(512)S(1)} %get-tuple-element.19, f32[512]{0:T(512)S(1)} %get-tuple-element.20), kind=kOutput, calls=%fused_computation.43 | convolution fusion | flops 3222536192 | bytes 4722688 | tf_op jit(solution)/shard_map/slkj,jy->slky/dot_general | solution.py:89
  221.8 4.5 %convolution_bitcast_fusion.1 = f32[1,4,256,512]{2,3,1,0:T(8,128)} fusion(f32[4,256,512]{1,2,0:T(8,128)S(1)} %fusion.19, f32[256]{0:T(256)S(1)} %get-tuple-element.17, f32[256]{0:T(256)S(1)} %get-tuple-element.18), kind=kOutput, calls=%fused_computation.46 | convolution fusion | flops 1610809344 | bytes 4196352 | tf_op jit(solution)/shard_map/kx,slky->slxy/dot_general | solution.py:90
  226.2 3.0 copy.50
  229.2 0.0 all-to-all-done.2
  229.2 7.8 %all-to-all-start.1 = ((f32[1,4,256,512]{3,1,0,2:T(4,128)}), f32[1,4,256,512]{3,1,0,2:T(4,128)}, u32[]{:S(2)}, u32[]{:S(2)}) async-start(f32[1,4,256,512]{3,1,0,2:T(4,128)} %copy.50), calls=%async_computation.1 | async-start | bytes 4194304 | tf_op jit(solution)/shard_map/all_to_all | solution.py:91
  237.1 4.4 %fusion.11 = f32[4,512,256]{2,1,0:T(8,128)S(1)} fusion(f32[1,4,32,8,512]{4,3,1,2,0:T(8,128)S(1)} %bitcast.78, f32[256]{0:T(256)S(1)} %get-tuple-element.17, f32[256]{0:T(256)S(1)} %get-tuple-element.18), kind=kOutput, calls=%fused_computation.33 | convolution fusion | flops 1610809344 | bytes 4196352 | tf_op jit(solution)/shard_map/kx,slxy->slky/dot_general | solution.py:86
  241.5 10.4 %fusion.7 = f32[4,256,512]{2,1,0:T(8,128)S(1)} fusion(f32[4,512,256]{2,1,0:T(8,128)S(1)} %fusion.11, f32[512]{0:T(512)S(1)} %get-tuple-element.19, f32[512]{0:T(512)S(1)} %get-tuple-element.20), kind=kOutput, calls=%fused_computation.29 | convolution fusion | flops 3222011904 | bytes 4198400 | tf_op jit(solution)/shard_map/slky,jy->slkj/dot_general | solution.py:87
  251.9 7.2 %fusion.17 = f32[4,256,512]{1,2,0:T(8,128)S(1)} fusion(f32[4,256,512]{2,1,0:T(8,128)S(1)} %fusion.7, f32[256,512]{1,0:T(8,128)S(1)} %copy-done.4, f32[512]{0:T(512)S(1)} %get-tuple-element.19, f32[512]{0:T(512)S(1)} %get-tuple-element.20), kind=kOutput, calls=%fused_computation.41 | convolution fusion | flops 3222536192 | bytes 4722688 | tf_op jit(solution)/shard_map/slkj,jy->slky/dot_general | solution.py:89
  259.1 3.0 convolution_bitcast_fusion
  262.1 2.0 copy.57
  264.0 0.0 all-to-all-done.1
  264.0 7.8 %all-to-all-start.3 = ((f32[1,4,256,512]{3,1,0,2:T(4,128)}), f32[1,4,256,512]{3,1,0,2:T(4,128)S(1)}, u32[]{:S(2)}, u32[]{:S(2)}) async-start(f32[1,4,256,512]{3,1,0,2:T(4,128)} %copy.57), calls=%async_computation.3 | async-start | bytes 4194304 | tf_op jit(solution)/shard_map/all_to_all | solution.py:91
  271.8 2.3 copy.102
  274.1 1.5 copy.52
  275.6 3.0 copy.60
  278.6 10.2 %all-to-all-done.3 = f32[1,4,256,512]{3,1,0,2:T(4,128)S(1)} async-done(((f32[1,4,256,512]{3,1,0,2:T(4,128)}), f32[1,4,256,512]{3,1,0,2:T(4,128)S(1)}, u32[]{:S(2)}, u32[]{:S(2)}) %all-to-all-start.3) | async-done | bytes 2097184 | tf_op jit(solution)/shard_map/all_to_all | solution.py:91
  288.8 0.7 copy.101
  289.5 0.2 copy.59
  289.7 1.9 copy.61
  291.6 0.0 copy-done
  291.6 6.5 %fusion.4 = f32[2,128,8,512]{1,3,2,0:T(8,128)} fusion(f32[1,128,8,512]{1,3,2,0:T(8,128)} %copy.61, f32[1,128,8,512]{1,3,2,0:T(8,128)} %copy.60, f32[128,128]{1,0:T(8,128)S(1)} %copy-done), kind=kOutput, calls=%fused_computation.27 | convolution fusion | flops 1611661312 | bytes 8454144 | tf_op jit(solution)/shard_map/ml,slxy->smxy/dot_general | solution.py:94
  298.0 5.4 %copy.62 = f32[2,128,8,512]{3,2,1,0:T(8,128)} copy(f32[2,128,8,512]{1,3,2,0:T(8,128)} %fusion.4) | data formatting | bytes 8388608 | tf_op jit(solution)/shard_map/ml,slxy->smxy/transpose | solution.py:94
  (3 shorter events, 0.0 us)
Async XLA Ops:
  0.0 291.6 %copy-start = (f32[128,128]{1,0:T(8,128)S(1)}, f32[128,128]{1,0:T(8,128)}, u32[]{:S(2)}) copy-start(f32[128,128]{1,0:T(8,128)} %param.9) | copy-start | bytes 196612
  4.6 18.7 %collective-permute-start = (f32[2,128,1,512]{3,2,0,1:T(1,128)S(1)}, f32[2,128,1,512]{3,2,0,1:T(1,128)S(1)}, u32[]{:S(2)}, u32[]{:S(2)}) collective-permute-start(f32[2,128,1,512]{3,2,0,1:T(1,128)S(1)} %get-tuple-element.16), channel_id=1, source_target_pairs={{1,0},{2,1},{3,2},{4,3},{5,4},{6,5},{7,6},{8,7},{9,8},{10,9},{11,1... | collective-permute-start | bytes 1572872 | tf_op jit(solution)/shard_map/ppermute | solution.py:20
  12.6 18.9 %copy-start.1 = (f32[2,128,8,512]{3,2,1,0:T(8,128)S(1)}, f32[2,128,8,512]{3,2,1,0:T(8,128)}, u32[]{:S(2)}) copy-start(f32[2,128,8,512]{3,2,1,0:T(8,128)} %param.6) | copy-start | bytes 12582916
  12.7 18.9 %copy-start.2 = (f32[2,128,8,512]{3,2,1,0:T(8,128)S(1)}, f32[2,128,8,512]{3,2,1,0:T(8,128)}, u32[]{:S(2)}) copy-start(f32[2,128,8,512]{3,2,1,0:T(8,128)} %param.7) | copy-start | bytes 12582916
  12.7 18.9 %collective-permute-start.1 = (f32[2,128,1,512]{3,2,0,1:T(1,128)S(1)}, f32[2,128,1,512]{3,2,0,1:T(1,128)S(1)}, u32[]{:S(2)}, u32[]{:S(2)}) collective-permute-start(f32[2,128,1,512]{3,2,0,1:T(1,128)S(1)} %get-tuple-element.15), channel_id=1, source_target_pairs={{0,1},{1,2},{2,3},{3,4},{4,5},{5,6},{6,7},{7,8},{8,9},{9,10},{10,1... | collective-permute-start | bytes 1572872 | tf_op jit(solution)/shard_map/ppermute | solution.py:19
  36.7 13.6 %collective-permute-start.2 = (f32[2,128,1,512]{3,2,0,1:T(1,128)S(1)}, f32[2,128,1,512]{3,2,0,1:T(1,128)S(1)}, u32[]{:S(2)}, u32[]{:S(2)}) collective-permute-start(f32[2,128,1,512]{3,2,0,1:T(1,128)S(1)} %get-tuple-element.14), channel_id=1, source_target_pairs={{1,0},{2,1},{3,2},{4,3},{5,4},{6,5},{7,6},{8,7},{9,8},{10,9},{11,1... | collective-permute-start | bytes 1572872 | tf_op jit(solution)/shard_map/ppermute | solution.py:20
  38.6 17.8 %collective-permute-start.3 = (f32[2,128,1,512]{3,2,0,1:T(1,128)S(1)}, f32[2,128,1,512]{3,2,0,1:T(1,128)S(1)}, u32[]{:S(2)}, u32[]{:S(2)}) collective-permute-start(f32[2,128,1,512]{3,2,0,1:T(1,128)S(1)} %get-tuple-element.13), channel_id=1, source_target_pairs={{0,1},{1,2},{2,3},{3,4},{4,5},{5,6},{6,7},{7,8},{8,9},{9,10},{10,1... | collective-permute-start | bytes 1572872 | tf_op jit(solution)/shard_map/ppermute | solution.py:19
  61.4 12.7 %collective-permute-start.4 = (f32[2,128,1,512]{3,2,0,1:T(1,128)S(1)}, f32[2,128,1,512]{3,2,0,1:T(1,128)S(1)}, u32[]{:S(2)}, u32[]{:S(2)}) collective-permute-start(f32[2,128,1,512]{3,2,0,1:T(1,128)S(1)} %get-tuple-element.12), channel_id=1, source_target_pairs={{1,0},{2,1},{3,2},{4,3},{5,4},{6,5},{7,6},{8,7},{9,8},{10,9},{11,1... | collective-permute-start | bytes 1572872 | tf_op jit(solution)/shard_map/ppermute | solution.py:20
  63.4 16.9 %collective-permute-start.5 = (f32[2,128,1,512]{3,2,0,1:T(1,128)S(1)}, f32[2,128,1,512]{3,2,0,1:T(1,128)S(1)}, u32[]{:S(2)}, u32[]{:S(2)}) collective-permute-start(f32[2,128,1,512]{3,2,0,1:T(1,128)S(1)} %get-tuple-element.11), channel_id=1, source_target_pairs={{0,1},{1,2},{2,3},{3,4},{4,5},{5,6},{6,7},{7,8},{8,9},{9,10},{10,1... | collective-permute-start | bytes 1572872 | tf_op jit(solution)/shard_map/ppermute | solution.py:19
  85.4 11.9 %collective-permute-start.6 = (f32[2,128,1,512]{3,2,0,1:T(1,128)S(1)}, f32[2,128,1,512]{3,2,0,1:T(1,128)S(1)}, u32[]{:S(2)}, u32[]{:S(2)}) collective-permute-start(f32[2,128,1,512]{3,2,0,1:T(1,128)S(1)} %get-tuple-element.10), channel_id=1, source_target_pairs={{1,0},{2,1},{3,2},{4,3},{5,4},{6,5},{7,6},{8,7},{9,8},{10,9},{11,1... | collective-permute-start | bytes 1572872 | tf_op jit(solution)/shard_map/ppermute | solution.py:20
  87.3 16.1 %collective-permute-start.7 = (f32[2,128,1,512]{3,2,0,1:T(1,128)S(1)}, f32[2,128,1,512]{3,2,0,1:T(1,128)S(1)}, u32[]{:S(2)}, u32[]{:S(2)}) collective-permute-start(f32[2,128,1,512]{3,2,0,1:T(1,128)S(1)} %get-tuple-element.9), channel_id=1, source_target_pairs={{0,1},{1,2},{2,3},{3,4},{4,5},{5,6},{6,7},{7,8},{8,9},{9,10},{10,1... | collective-permute-start | bytes 1572872 | tf_op jit(solution)/shard_map/ppermute | solution.py:19
  107.8 43.2 %copy-start.3 = (f32[2,128,8,512]{3,2,1,0:T(8,128)S(1)}, f32[2,128,8,512]{3,2,1,0:T(8,128)}, u32[]{:S(2)}) copy-start(f32[2,128,8,512]{3,2,1,0:T(8,128)} %param.5) | copy-start | bytes 12582916
  108.3 42.6 %collective-permute-start.8 = (f32[128,8,512]{2,1,0:T(8,128)S(1)}, f32[128,8,512]{2,1,0:T(8,128)S(1)}, u32[]{:S(2)}, u32[]{:S(2)}) collective-permute-start(f32[128,8,512]{2,1,0:T(8,128)S(1)} %get-tuple-element.7), channel_id=1, source_target_pairs={{0,32},{32,64},{64,96},{1,33},{33,65},{65,97},{2,34},{34,66},{66,9... | collective-permute-start | bytes 6291464 | tf_op jit(solution)/shard_map/ppermute | solution.py:28
  184.5 44.7 %all-to-all-start.2 = ((f32[1,128,8,512]{3,2,0,1:T(8,128)}), f32[1,128,8,512]{3,2,0,1:T(8,128)S(1)}, u32[]{:S(2)}, u32[]{:S(2)}) async-start(f32[1,128,8,512]{3,2,0,1:T(8,128)} %get-tuple-element.6), calls=%async_computation.2 | async-start | bytes 4194304 | tf_op jit(solution)/shard_map/all_to_all | solution.py:34
  189.5 25.1 %copy-start.4 = (f32[256,512]{1,0:T(8,128)S(1)}, f32[256,512]{1,0:T(8,128)}, u32[]{:S(2)}) copy-start(f32[256,512]{1,0:T(8,128)} %param.8) | copy-start | bytes 1572868
  229.2 34.8 %all-to-all-start.1 = ((f32[1,4,256,512]{3,1,0,2:T(4,128)}), f32[1,4,256,512]{3,1,0,2:T(4,128)}, u32[]{:S(2)}, u32[]{:S(2)}) async-start(f32[1,4,256,512]{3,1,0,2:T(4,128)} %copy.50), calls=%async_computation.1 | async-start | bytes 4194304 | tf_op jit(solution)/shard_map/all_to_all | solution.py:91
  264.0 24.8 %all-to-all-start.3 = ((f32[1,4,256,512]{3,1,0,2:T(4,128)}), f32[1,4,256,512]{3,1,0,2:T(4,128)S(1)}, u32[]{:S(2)}, u32[]{:S(2)}) async-start(f32[1,4,256,512]{3,1,0,2:T(4,128)} %copy.57), calls=%async_computation.3 | async-start | bytes 4194304 | tf_op jit(solution)/shard_map/all_to_all | solution.py:91
where the time goes:
time: 309 us; the launch traced here: 304 us
  waiting for transfers between devices  98.6 us (32%)
  matrix products  68.1 us (22%)
  starting transfers between devices  55.4 us (18%)
  local copies, waits for them, and re-layouts  31.6 us (10%)
  blocking collectives  30.8 us (10%)
  other arithmetic  18.6 us (6%)
    ppermute x1, waiting for transfers between devices, shifted(): return lax.ppermute(value, axis, pairs)  33.9 us
    all_to_all x1, blocking collectives, moved(): lax.all_to_all(group, axis, split_axis=split_dim, concat_axis=concat_dim,...  30.8 us
    dot_general x2, matrix products, planes(): forward = jnp.einsum('slky,jy->slkj', forward, col_table, precision=high)  29.4 us
    ppermute x4, waiting for transfers between devices, extended_2(): after = lax.ppermute(initial, axis, down)  27.7 us
    ppermute x4, waiting for transfers between devices, extended_2(): before = lax.ppermute(last, axis, up)  26.8 us
    add x4, other arithmetic, advance(): center - 0.5 * courant_x * (north - south) - 0.5 * courant_y * (east - west)  17.6 us
    all_to_all x2, starting transfers between devices, planes(): lax.all_to_all(back, 'brick', split_axis=2, concat_axis=1, tiled=True)  15.6 us
    dot_general x2, matrix products, planes(): back = jnp.einsum('slkj,jy->slky', scaled, col_table, precision=high)  14.4 us
  transfers between devices with their start and end apart: 12, of which 10 were waited for; matrix products, arithmetic and copies ran while one was open for 25% of the time, Pallas kernels for 0%

commit v1 on v0

v1 whole, which is shorter than its diff:
```python
import jax
import jax.numpy as jnp
import ml_dtypes
import numpy as np
from jax import lax
from jax.experimental import pallas as pl
from jax.experimental.pallas import tpu as pltpu
from jax.sharding import PartitionSpec as P

STEPS = 4
ROWS, LEVELS, COLS, NX = 8, 128, 512, 256
MESH = pl.DeviceIdType.MESH
F32, BF16 = jnp.float32, jnp.bfloat16
EVEN, ODD_A, ODD_B = (0, 0, 128), (1, 0, 64), (1, 64, 64)
STREAMS = (EVEN, ODD_A, ODD_B)
XZ_ORDER = ((1, 0), (0, 1), (1, 1), (0, 3), (1, 3), (0, 2), (1, 2))


def dct_table(count):
    one = np.float32
    freq = np.arange(count, dtype=one)[:, None]
    cells = np.arange(count, dtype=one)[None, :]
    angle = one(np.pi) * (cells + one(0.5)) * freq / one(count)
    table = np.cos(angle.astype(np.float64)).astype(one) * np.sqrt(one(2.0) / one(count))
    table[0] *= np.sqrt(one(0.5))
    return table


def halves(table):
    high = table.astype(ml_dtypes.bfloat16)
    low = (table - high.astype(np.float32)).astype(ml_dtypes.bfloat16)
    return np.stack([high, low])


def split(value):
    high = value.astype(BF16)
    return high, (value - high.astype(F32)).astype(BF16)


def product(a, b):
    def dot(u, v):
        return jnp.dot(u, v, preferred_element_type=F32)

    return dot(a[0], b[0]) + (dot(a[0], b[1]) + dot(a[1], b[0]))


def kernel(
    inc_hbm, cx_hbm, cy_hbm, spec_hbm, vert_hbm, rt_hbm, rtt_hbm, ct_hbm, ctt_hbm,
    out_hbm,
    inc, cx, cy, one_buf, two_buf, halo, prior, jumps, mid, planes, mid_back, done,
    spec, vert, rt, rtt, ct, ctt,
    load_sem, table_sem, halo_send, halo_recv, prior_send, prior_recv,
    a_send, a_recv, b_send, b_recv, c_send, c_recv, d_send, d_recv, out_sem,
):
    sub, brick = lax.axis_index("sub"), lax.axis_index("brick")
    x, z, y = brick // 16, lax.rem(brick // 4, 4), lax.rem(brick, 4)
    mine = x * 4 + z
    up, down = lax.rem(brick + 1, 32), lax.rem(brick + 31, 32)
    keep_up = jnp.where(brick == 31, 0.0, 1.0).astype(F32)
    keep_down = jnp.where(brick == 0, 0.0, 1.0).astype(F32)

    def xz_peer(dx, dz):
        px, pz = lax.rem(x + dx, 2), lax.rem(z + dz, 4)
        return px * 4 + pz, {"brick": px * 16 + pz * 4 + y}

    def y_peer(dy):
        py = lax.rem(y + dy, 4)
        return py, {"brick": brick - y + py}

    def remote(src, dst, send, recv, device):
        return pltpu.make_async_remote_copy(
            src_ref=src, dst_ref=dst, send_sem=send, recv_sem=recv, device_id=device, device_id_type=MESH
        )

    loads = {}

    def load(name, src, dst, s, rows):
        for r in rows:
            copy = pltpu.make_async_copy(src.at[s, :, r, :], dst.at[s, r], load_sem.at[len(loads)])
            copy.start()
            loads[name, s, r] = copy

    edges, inner = (0, 7), tuple(range(1, 7))
    for s in (0, 1):
        load("inc", inc_hbm, inc, s, edges)
    load("inc", inc_hbm, inc, 0, inner)
    load("cx", cx_hbm, cx, 0, edges + inner)
    load("cy", cy_hbm, cy, 0, edges + inner)
    load("inc", inc_hbm, inc, 1, inner)
    load("cx", cx_hbm, cx, 1, edges + inner)
    load("cy", cy_hbm, cy, 1, edges + inner)
    tables = [
        pltpu.make_async_copy(src, dst, table_sem.at[i])
        for i, (src, dst) in enumerate(
            ((vert_hbm, vert), (spec_hbm, spec), (rt_hbm, rt), (rtt_hbm, rtt), (ct_hbm, ct), (ctt_hbm, ctt))
        )
    ]
    for copy in tables:
        copy.start()

    barrier = pltpu.get_barrier_semaphore()
    peers = [{"brick": up}, {"brick": down}, {"sub": lax.rem(sub + 1, 4)}, {"sub": lax.rem(sub + 3, 4)}]
    peers += [xz_peer(dx, dz)[1] for dx, dz in XZ_ORDER] + [y_peer(dy)[1] for dy in (1, 2, 3)]
    for peer in peers:
        pl.semaphore_signal(barrier, inc=1, device_id=peer, device_id_type=MESH)

    pl.semaphore_wait(barrier, len(peers))

    def state(step):
        return inc if step == 0 else (one_buf if step % 2 else two_buf)

    def halo_copies(stream, step):
        s, low, count = stream
        n, t = STREAMS.index(stream), step - 1
        levels = pl.ds(low, count)
        src = state(step - 1)
        return (
            remote(src.at[s, 7, levels], halo.at[s, t, 0, levels], halo_send.at[n, t, 0], halo_recv.at[n, t, 0], {"brick": up}),
            remote(src.at[s, 0, levels], halo.at[s, t, 1, levels], halo_send.at[n, t, 1], halo_recv.at[n, t, 1], {"brick": down}),
        )

    def rows(stream, step, which, block):
        s, low, count = stream
        src, dst = state(step - 1), state(step)
        lane = lax.broadcasted_iota(jnp.int32, (block, COLS), 1)

        def body(i, carry):
            at = pl.ds(pl.multiple_of(low + i * block, 8), block)
            for r in which:
                center = src[s, r, at]
                north = src[s, r + 1, at] if r < 7 else halo[s, step - 1, 1, at] * keep_up
                south = src[s, r - 1, at] if r > 0 else halo[s, step - 1, 0, at] * keep_down
                east = jnp.where(lane == COLS - 1, 0.0, pltpu.roll(center, COLS - 1, 1))
                west = jnp.where(lane == 0, 0.0, pltpu.roll(center, 1, 1))
                flow = cx[s, r, at] * (north - south) + cy[s, r, at] * (east - west)
                spread = (north + south) + (east + west) - 4.0 * center
                dst[s, r, at] = center - 0.5 * flow + 0.2 * spread
            return carry

        lax.fori_loop(0, count // block, body, 0)

    def event(stream, step):
        s, low, count = stream
        for copy in halo_copies(stream, step):
            copy.wait_recv()
        if step >= 3:
            for copy in halo_copies(stream, step - 1):
                copy.wait_send()
        rows(stream, step, edges, 16)
        if step < STEPS:
            for copy in halo_copies(stream, step + 1):
                copy.start()
        rows(stream, step, inner, 8)

    def start_chunks(s, ends, first):
        weights = split(vert[...])
        for r in range(ROWS):
            mixed = product(weights, split(inc[s, r] - ends[r]))
            for c in range(4):
                jumps[first + c, :, r, :] = mixed[32 * c : 32 * c + 32]
        for c in range(4):
            k = first + c
            for dx, dz in XZ_ORDER:
                there, device = xz_peer(dx, dz)
                remote(jumps.at[k, pl.ds(there * 4, 4)], mid.at[k, mine], a_send.at[k], a_recv.at[k], device).start()

    def a_all(k):
        part = mid.at[k, pl.ds(0, 7)]
        return remote(part, part, a_send.at[k], a_recv.at[k], {"brick": up})

    def b_all(k):
        return remote(planes.at[k, pl.ds(0, 6)], planes.at[k, pl.ds(0, 6)], b_send.at[k], b_recv.at[k], {"brick": up})

    def c_all(k):
        return remote(mid_back.at[k, pl.ds(0, 6)], mid_back.at[k, pl.ds(0, 6)], c_send.at[k], c_recv.at[k], {"brick": up})

    def d_all(k):
        return remote(done.at[k, pl.ds(0, 28)], done.at[k, pl.ds(0, 28)], d_send.at[k], d_recv.at[k], {"brick": up})

    def second_hop(k):
        a_all(k).wait_recv()
        mid[k, mine] = jumps[k, pl.ds(mine * 4, 4)]
        for dy in (1, 3, 2):
            there, device = y_peer(dy)
            remote(mid.at[k, :, there], planes.at[k, :, y], b_send.at[k], b_recv.at[k], device).start()
        planes[k, :, y] = mid[k, :, y]

    def transform(k):
        b_all(k).wait_recv()
        plane = planes[k].reshape(NX, COLS)
        value = product((rt[0], rt[1]), split(plane))
        value = product(split(value), (ctt[0], ctt[1])) * spec[...]
        value = product(split(value), (ct[0], ct[1]))
        value = product((rtt[0], rtt[1]), split(value))
        planes[k] = value.reshape(8, 4, ROWS, COLS)
        for dy in (1, 3, 2):
            there, device = y_peer(dy)
            remote(planes.at[k, :, there], mid_back.at[k, :, y], c_send.at[k], c_recv.at[k], device).start()
        mid_back[k, :, y] = planes[k, :, y]

    def fourth_hop(k):
        c_all(k).wait_recv()
        for dx, dz in XZ_ORDER:
            there, device = xz_peer(dx, dz)
            remote(mid_back.at[k, there], done.at[k, pl.ds(mine * 4, 4)], d_send.at[k], d_recv.at[k], device).start()
        done[k, pl.ds(mine * 4, 4)] = mid_back[k, mine]

    def out_copy(k):
        s, c = (1, k) if k < 4 else (0, k - 4)
        return pltpu.make_async_copy(done.at[k], out_hbm.at[s, pl.ds(32 * c, 32)], out_sem.at[k])

    def finish(k):
        d_all(k).wait_recv()
        out_copy(k).start()

    for s in (0, 1):
        for r in edges:
            loads["inc", s, r].wait()
        for stream in STREAMS:
            if stream[0] == s:
                for copy in halo_copies(stream, 1):
                    copy.start()
    for s in (0, 1):
        for r in inner:
            loads["inc", s, r].wait()
        for r in range(ROWS):
            loads["cx", s, r].wait()
            loads["cy", s, r].wait()
        if s == 0:
            event(EVEN, 1)
    event(ODD_A, 1)
    event(EVEN, 2)
    event(ODD_B, 1)
    event(EVEN, 3)
    event(ODD_A, 2)
    event(EVEN, 4)
    event(ODD_B, 2)
    tables[0].wait()
    start_chunks(1, two_buf.at[0], 0)
    event(ODD_A, 3)
    event(ODD_B, 3)

    def prior_copy(stream):
        s, low, count = stream
        n = STREAMS.index(stream) - 1
        levels = pl.ds(low, count)
        return remote(
            two_buf.at[1, :, levels], prior.at[:, levels], prior_send.at[n], prior_recv.at[n], {"sub": lax.rem(sub + 1, 4)}
        )

    for stream in (ODD_A, ODD_B):
        event(stream, 4)

        @pl.when(sub < 3)
        def _():
            prior_copy(stream).start()

    @pl.when(sub == 0)
    def _():
        prior[...] = jnp.zeros(prior.shape, F32)

    for copy in tables[1:]:
        copy.wait()
    for k in range(4):
        second_hop(k)

    def odd_planes(k, carry):
        transform(k)
        return carry

    lax.fori_loop(0, 4, odd_planes, 0)

    @pl.when(sub > 0)
    def _():
        for stream in (ODD_A, ODD_B):
            prior_copy(stream).wait_recv()

    start_chunks(0, prior, 4)
    for k in range(4):
        fourth_hop(k)
        second_hop(k + 4)

    def even_planes(k, carry):
        transform(k)
        return carry

    lax.fori_loop(4, 8, even_planes, 0)
    for k in range(4):
        finish(k)
    for k in range(4, 8):
        fourth_hop(k)
    for k in range(4, 8):
        finish(k)

    for stream in STREAMS:
        for step in (1, STEPS):
            for copy in halo_copies(stream, step):
                copy.wait_send()

    @pl.when(sub < 3)
    def _():
        for stream in (ODD_A, ODD_B):
            prior_copy(stream).wait_send()

    for k in range(8):
        a_all(k).wait_send()
        b_all(k).wait_send()
        c_all(k).wait_send()
        d_all(k).wait_send()
        out_copy(k).wait()


def on_device(increments, courant_x, courant_y, spectrum, vertical):
    row_table, col_table = dct_table(NX), dct_table(COLS)
    tables = [halves(t) for t in (row_table, row_table.T, col_table, col_table.T)]
    hbm = pl.BlockSpec(memory_space=pl.ANY)
    slabs = (2, ROWS, LEVELS, COLS)
    dma = pltpu.SemaphoreType.DMA
    return pl.pallas_call(
        kernel,
        out_shape=jax.ShapeDtypeStruct((2, LEVELS, ROWS, COLS), F32),
        in_specs=[hbm] * 9,
        out_specs=hbm,
        scratch_shapes=[
            pltpu.VMEM(slabs, F32),
            pltpu.VMEM(slabs, F32),
            pltpu.VMEM(slabs, F32),
            pltpu.VMEM(slabs, F32),
            pltpu.VMEM(slabs, F32),
            pltpu.VMEM((2, STEPS, 2, LEVELS, COLS), F32),
            pltpu.VMEM((ROWS, LEVELS, COLS), F32),
            pltpu.VMEM((8, 32, ROWS, COLS), F32),
            pltpu.VMEM((8, 8, 4, ROWS, COLS), F32),
            pltpu.VMEM((8, 8, 4, ROWS, COLS), F32),
            pltpu.VMEM((8, 8, 4, ROWS, COLS), F32),
            pltpu.VMEM((8, 32, ROWS, COLS), F32),
            pltpu.VMEM((NX, COLS), F32),
            pltpu.VMEM((LEVELS, LEVELS), F32),
            pltpu.VMEM((2, NX, NX), BF16),
            pltpu.VMEM((2, NX, NX), BF16),
            pltpu.VMEM((2, COLS, COLS), BF16),
            pltpu.VMEM((2, COLS, COLS), BF16),
            dma((48,)),
            dma((6,)),
            dma((3, STEPS, 2)),
            dma((3, STEPS, 2)),
            dma((2,)),
            dma((2,)),
            *[dma((8,)) for _ in range(9)],
        ],
        compiler_params=pltpu.CompilerParams(
            collective_id=0, has_side_effects=True, vmem_limit_bytes=67_043_328
        ),
    )(increments, courant_x, courant_y, spectrum, vertical, *[jnp.asarray(t) for t in tables])


def solution(mesh):
    wide = P("sub", None, "brick", None)
    return jax.shard_map(
        on_device, mesh=mesh, in_specs=(wide, wide, wide, P(), P()), out_specs=wide, check_vma=False
    )
```

time: 309 us -> 187 us (0.61)
  the two profiles are of different devices: /device:TPU:3 before, /device:TPU:80 now
where the time goes in v1:
time: 187 us
  Pallas kernels  182 us (97%)
  local copies, waits for them, and re-layouts  4.64 us (2%)
    pallas_call x1, Pallas kernels, on_device(): pl.pallas_call(kernel, out_shape=jax.ShapeDtypeStruct((2, LEVELS, ROWS, C...  182 us
    unnamed x1, local copies, waits for them, and re-layouts  4.64 us

profile of v1, /device:TPU:80, one launch (start us, length us, event | category | flops | bytes accessed | tf_op | source)
XLA Modules:
  0.0 187.0 jit_solution(7772640880398555628)
XLA Ops:
  0.0 182.4 %shard_map.91 = f32[2,128,8,512]{3,2,1,0:T(8,128)} custom-call(f32[2,128,8,512]{3,2,1,0:T(8,128)} %inc_hbm.1, f32[2,128,8,512]{3,2,1,0:T(8,128)} %cx_hbm.1, f32[2,128,8,512]{3,2,1,0:T(8,128)} %cy_hbm.1, f32[256,512]{1,0:T(8,128)} %spec_hbm.1, f32[128,128]{1,0:T(8,128)} %vert_hbm.1, bf16[2,256,256]{2,1,0:T(8,128)(2,1)} %constant.8.clone.rt_hbm, ...), custom_call_target="tpu_custom_call" | custom-call | tf_op jit(solution)/shard_map/pallas_call | solution.py:319
  182.4 4.6 %copy.11 = f32[2,128,8,512]{3,2,1,0:T(8,128)} copy(f32[2,128,8,512]{3,2,1,0:T(8,128)} %shard_map.91) | data formatting | bytes 8388608

commit v2 on v1

v2 whole, which is shorter than its diff:
```python
import jax
import jax.numpy as jnp
import ml_dtypes
import numpy as np
from jax import lax
from jax.experimental import pallas as pl
from jax.experimental.pallas import tpu as pltpu
from jax.sharding import PartitionSpec as P

STEPS = 4
ROWS, LEVELS, COLS, NX = 8, 128, 512, 256
MESH = pl.DeviceIdType.MESH
F32, BF16 = jnp.float32, jnp.bfloat16
CHUNKS, CHUNK = 8, 32
XZ_ORDER = ((1, 0), (0, 1), (1, 1), (0, 3), (1, 3), (0, 2), (1, 2))


def dct_table(count):
    one = np.float32
    freq = np.arange(count, dtype=one)[:, None]
    cells = np.arange(count, dtype=one)[None, :]
    angle = one(np.pi) * (cells + one(0.5)) * freq / one(count)
    table = np.cos(angle.astype(np.float64)).astype(one) * np.sqrt(one(2.0) / one(count))
    table[0] *= np.sqrt(one(0.5))
    return table


def halves(table):
    high = table.astype(ml_dtypes.bfloat16)
    low = (table - high.astype(np.float32)).astype(ml_dtypes.bfloat16)
    return np.stack([high, low])


def split(value):
    high = value.astype(BF16)
    return high, (value - high.astype(F32)).astype(BF16)


def product(a, b):
    def dot(u, v):
        return jnp.dot(u, v, preferred_element_type=F32)

    return dot(a[0], b[0]) + (dot(a[0], b[1]) + dot(a[1], b[0]))


def kernel(
    inc_hbm, cx_hbm, cy_hbm, spec_hbm, rt_hbm, rtt_hbm, ct_hbm, ctt_hbm,
    out_hbm,
    inc, cx, cy, one_buf, two_buf, halo, prior, jumps, mid, planes, mid_back, done,
    spec, rt, rtt, ct, ctt,
    load_sem, table_sem, halo_send, halo_recv, prior_send, prior_recv,
    a_send, a_recv, b_send, b_recv, c_send, c_recv, d_send, d_recv, out_sem,
):
    sub, brick = lax.axis_index("sub"), lax.axis_index("brick")
    x, z, y = brick // 16, lax.rem(brick // 4, 4), lax.rem(brick, 4)
    mine = x * 4 + z
    up, down = lax.rem(brick + 1, 32), lax.rem(brick + 31, 32)

    def xz_peer(dx, dz):
        px, pz = lax.rem(x + dx, 2), lax.rem(z + dz, 4)
        return px * 4 + pz, {"brick": px * 16 + pz * 4 + y}

    def y_peer(dy):
        py = lax.rem(y + dy, 4)
        return py, {"brick": brick - y + py}

    def remote(src, dst, send, recv, device):
        return pltpu.make_async_remote_copy(
            src_ref=src, dst_ref=dst, send_sem=send, recv_sem=recv, device_id=device, device_id_type=MESH
        )

    loads = []

    def load(src, dst, s, rows):
        for r in rows:
            copy = pltpu.make_async_copy(src.at[s, :, r, :], dst.at[s, r], load_sem.at[len(loads)])
            copy.start()
            loads.append(copy)

    edges, inner = (0, 7), tuple(range(1, 7))
    for s in (1, 0):
        load(inc_hbm, inc, s, edges)
    for s in (1, 0):
        load(inc_hbm, inc, s, inner)
        load(cx_hbm, cx, s, edges + inner)
        load(cy_hbm, cy, s, edges + inner)
    tables = [
        pltpu.make_async_copy(src, dst, table_sem.at[i])
        for i, (src, dst) in enumerate(
            ((spec_hbm, spec), (rt_hbm, rt), (rtt_hbm, rtt), (ct_hbm, ct), (ctt_hbm, ctt))
        )
    ]
    for copy in tables:
        copy.start()

    barrier = pltpu.get_barrier_semaphore()
    peers = [{"brick": up}, {"brick": down}, {"sub": lax.rem(sub + 1, 4)}, {"sub": lax.rem(sub + 3, 4)}]
    peers += [xz_peer(dx, dz)[1] for dx, dz in XZ_ORDER] + [y_peer(dy)[1] for dy in (1, 2, 3)]
    for peer in peers:
        pl.semaphore_signal(barrier, inc=1, device_id=peer, device_id_type=MESH)

    pl.semaphore_wait(barrier, len(peers))

    def state(step):
        return inc if step == 0 else (one_buf if step % 2 else two_buf)

    def place(i):
        return 1 - lax.rem(i, 2), pl.multiple_of((i // 2) * CHUNK, CHUNK)

    def halo_copies(i, step):
        s, low = place(i)
        t, src, levels = step - 1, state(step - 1), pl.ds(low, CHUNK)
        return (
            remote(src.at[s, 7, levels], halo.at[s, t, 0, levels], halo_send.at[i, t, 0], halo_recv.at[i, t, 0], {"brick": up}),
            remote(src.at[s, 0, levels], halo.at[s, t, 1, levels], halo_send.at[i, t, 1], halo_recv.at[i, t, 1], {"brick": down}),
        )

    def halo_do(i, step, verb):
        live = jnp.logical_or(sub < 3, lax.rem(i, 2) == 1)
        upward, downward = halo_copies(i, step)
        below, above = (upward, downward) if verb == "wait_recv" else (downward, upward)
        pl.when(jnp.logical_and(live, brick > 0))(lambda: getattr(below, verb)())
        pl.when(jnp.logical_and(live, brick < 31))(lambda: getattr(above, verb)())

    def rows(i, step, which, block):
        s, low = place(i)
        src, dst = state(step - 1), state(step)
        lane = lax.broadcasted_iota(jnp.int32, (block, COLS), 1)

        def body(n, carry):
            at = pl.ds(pl.multiple_of(low + n * block, 8), block)
            for r in which:
                center = src[s, r, at]
                north = src[s, r + 1, at] if r < 7 else halo[s, step - 1, 1, at]
                south = src[s, r - 1, at] if r > 0 else halo[s, step - 1, 0, at]
                east = jnp.where(lane == COLS - 1, 0.0, pltpu.roll(center, COLS - 1, 1))
                west = jnp.where(lane == 0, 0.0, pltpu.roll(center, 1, 1))
                flow = cx[s, r, at] * (north - south) + cy[s, r, at] * (east - west)
                spread = (north + south) + (east + west) - 4.0 * center
                dst[s, r, at] = center - 0.5 * flow + 0.2 * spread
            return carry

        lax.fori_loop(0, CHUNK // block, body, 0)

    def edge_event(i, step):
        halo_do(i, step, "wait_recv")
        if step >= 3:
            halo_do(i, step - 1, "wait_send")
        rows(i, step, edges, 16)
        if step < STEPS:
            halo_do(i, step + 1, "start")

    def inner_event(i, step):
        rows(i, step, inner, 8)

    def prior_copy(i):
        levels = pl.ds(place(i)[1], CHUNK)
        return remote(
            two_buf.at[1, :, levels], prior.at[:, levels], prior_send.at[i // 2], prior_recv.at[i // 2],
            {"sub": lax.rem(sub + 1, 4)},
        )

    def start_chunk(k, s, ends):
        levels = pl.ds(place(k)[1], CHUNK)
        for r in range(ROWS):
            jumps[k, :, r, :] = inc[s, r, levels] - ends[r, levels]
        for dx, dz in XZ_ORDER:
            there, device = xz_peer(dx, dz)
            remote(jumps.at[k, pl.ds(there * 4, 4)], mid.at[k, mine], a_send.at[k], a_recv.at[k], device).start()

    def a_all(k):
        part = mid.at[k, pl.ds(0, 7)]
        return remote(part, part, a_send.at[k], a_recv.at[k], {"brick": up})

    def b_all(k):
        return remote(planes.at[k, pl.ds(0, 6)], planes.at[k, pl.ds(0, 6)], b_send.at[k], b_recv.at[k], {"brick": up})

    def c_all(k):
        return remote(mid_back.at[k, pl.ds(0, 7)], mid_back.at[k, pl.ds(0, 7)], c_send.at[k], c_recv.at[k], {"brick": up})

    def d_all(k):
        return remote(done.at[k, pl.ds(0, 6)], done.at[k, pl.ds(0, 6)], d_send.at[k], d_recv.at[k], {"brick": up})

    def second_hop(k):
        a_all(k).wait_recv()
        mid[k, mine] = jumps[k, pl.ds(mine * 4, 4)]
        for dy in (1, 3, 2):
            there, device = y_peer(dy)
            remote(mid.at[k, :, there], planes.at[k, :, y], b_send.at[k], b_recv.at[k], device).start()
        planes[k, :, y] = mid[k, :, y]

    def transform(k):
        b_all(k).wait_recv()
        plane = planes[k].reshape(NX, COLS)
        value = product((rt[0], rt[1]), split(plane))
        value = product(split(value), (ctt[0], ctt[1])) * spec[...]
        value = product(split(value), (ct[0], ct[1]))
        value = product((rtt[0], rtt[1]), split(value))
        planes[k] = value.reshape(8, 4, ROWS, COLS)
        for dx, dz in XZ_ORDER:
            there, device = xz_peer(dx, dz)
            remote(planes.at[k, there], mid_back.at[k, mine], c_send.at[k], c_recv.at[k], device).start()
        mid_back[k, mine] = planes[k, mine]

    def fourth_hop(k):
        c_all(k).wait_recv()
        for dy in (1, 3, 2):
            there, device = y_peer(dy)
            remote(mid_back.at[k, :, there], done.at[k, :, y], d_send.at[k], d_recv.at[k], device).start()
        done[k, :, y] = mid_back[k, :, y]

    def out_copy(k):
        return pltpu.make_async_copy(done.at[k], out_hbm.at[1 - lax.rem(k, 2), k // 2], out_sem.at[k])

    def finish(k):
        d_all(k).wait_recv()
        out_copy(k).start()

    for copy in loads[:4]:
        copy.wait()
    for i in range(3):
        halo_do(i, 1, "start")

    @pl.when(brick == 0)
    def _():
        halo[:, :, 0] = jnp.zeros((2, STEPS, LEVELS, COLS), F32)

    @pl.when(brick == 31)
    def _():
        halo[:, :, 1] = jnp.zeros((2, STEPS, LEVELS, COLS), F32)

    @pl.when(sub == 0)
    def _():
        prior[...] = jnp.zeros(prior.shape, F32)

    for copy in loads[4:]:
        copy.wait()
    for copy in tables:
        copy.wait()

    def each_round(j, carry):
        def within(i):
            return jnp.logical_and(i >= 0, i < CHUNKS)

        def stage(i, work, also=True):
            pl.when(jnp.logical_and(within(i), also))(lambda: work(i))

        def ahead(i):
            halo_do(i, 1, "start")

        def from_prior(k):
            pl.when(sub > 0)(lambda: prior_copy(k - 1).wait_recv())
            start_chunk(k, 0, prior)

        even, odd = lax.rem(j, 2) == 0, lax.rem(j, 2) == 1
        for step in range(STEPS, 0, -1):
            stage(j - step + 1, lambda i, step=step: edge_event(i, step))
        stage(j + 3, ahead)
        stage(j - 3, lambda i: inner_event(i, 4))
        stage(j - 3, lambda i: prior_copy(i).start(), jnp.logical_and(odd, sub < 3))
        stage(j - 4, lambda k: start_chunk(k, 1, two_buf.at[0]), even)
        stage(j - 4, from_prior, odd)
        for step in range(STEPS - 1, 0, -1):
            stage(j - step + 1, lambda i, step=step: inner_event(i, step))
        stage(j - 6, second_hop)
        stage(j - 7, transform)
        stage(j - 8, fourth_hop)
        stage(j - 11, finish)
        return carry

    lax.fori_loop(0, CHUNKS + 11, each_round, 0)

    def drain(k, carry):
        for step in (1, STEPS):
            halo_do(k, step, "wait_send")
        a_all(k).wait_send()
        b_all(k).wait_send()
        c_all(k).wait_send()
        d_all(k).wait_send()
        out_copy(k).wait()
        return carry

    lax.fori_loop(0, CHUNKS, drain, 0)

    @pl.when(sub < 3)
    def _():
        for c in range(4):
            prior_copy(2 * c).wait_send()


def vertical_kernel(h_hbm, v_ref, out_hbm, source, result, in_sem, out_sem):
    units = [(s, r) for s in range(2) for r in range(ROWS)]
    reads = [pltpu.make_async_copy(h_hbm.at[s, :, r, :], source.at[s, r], in_sem.at[s, r]) for s, r in units]
    writes = [pltpu.make_async_copy(result.at[s, r], out_hbm.at[s, :, r, :], out_sem.at[s, r]) for s, r in units]
    for copy in reads:
        copy.start()
    high, low = split(v_ref[...])
    wide = jnp.concatenate([high, low], axis=1)
    for first in range(0, len(units), 4):
        for copy in reads[first : first + 4]:
            copy.wait()
        for s, r in units[first : first + 4]:
            top, rest = split(source[s, r])
            result[s, r] = jnp.dot(
                wide, jnp.concatenate([top, top], axis=0), preferred_element_type=F32
            ) + jnp.dot(high, rest, preferred_element_type=F32)
        for copy in writes[first : first + 4]:
            copy.start()
    for copy in writes:
        copy.wait()


def on_device(increments, courant_x, courant_y, spectrum, vertical):
    row_table, col_table = dct_table(NX), dct_table(COLS)
    tables = [halves(t) for t in (row_table, row_table.T, col_table, col_table.T)]
    hbm = pl.BlockSpec(memory_space=pl.ANY)
    slabs = (2, ROWS, LEVELS, COLS)
    dma = pltpu.SemaphoreType.DMA
    whole = jax.ShapeDtypeStruct((2, LEVELS, ROWS, COLS), F32)
    horizontal = pl.pallas_call(
        kernel,
        out_shape=jax.ShapeDtypeStruct((2, 4, 8, 4, ROWS, COLS), F32),
        in_specs=[hbm] * 8,
        out_specs=hbm,
        scratch_shapes=[
            *[pltpu.VMEM(slabs, F32) for _ in range(5)],
            pltpu.VMEM((2, STEPS, 2, LEVELS, COLS), F32),
            pltpu.VMEM((ROWS, LEVELS, COLS), F32),
            pltpu.VMEM((CHUNKS, 32, ROWS, COLS), F32),
            *[pltpu.VMEM((CHUNKS, 8, 4, ROWS, COLS), F32) for _ in range(4)],
            pltpu.VMEM((NX, COLS), F32),
            *[pltpu.VMEM((2, NX, NX), BF16) for _ in range(2)],
            *[pltpu.VMEM((2, COLS, COLS), BF16) for _ in range(2)],
            dma((48,)),
            dma((5,)),
            *[dma((CHUNKS, STEPS, 2)) for _ in range(2)],
            *[dma((4,)) for _ in range(2)],
            *[dma((CHUNKS,)) for _ in range(9)],
        ],
        compiler_params=pltpu.CompilerParams(
            collective_id=0, has_side_effects=True, vmem_limit_bytes=67_043_328
        ),
    )(increments, courant_x, courant_y, spectrum, *[jnp.asarray(t) for t in tables])
    return pl.pallas_call(
        vertical_kernel,
        out_shape=whole,
        in_specs=[hbm, pl.BlockSpec(memory_space=pltpu.VMEM)],
        out_specs=hbm,
        scratch_shapes=[pltpu.VMEM(slabs, F32)] * 2 + [dma((2, ROWS))] * 2,
        compiler_params=pltpu.CompilerParams(vmem_limit_bytes=67_043_328),
    )(horizontal.reshape(whole.shape), vertical)


def solution(mesh):
    wide = P("sub", None, "brick", None)
    return jax.shard_map(
        on_device, mesh=mesh, in_specs=(wide, wide, wide, P(), P()), out_specs=wide, check_vma=False
    )
```

time: 187 us -> 199 us (1.064)
  the two profiles are of different devices: /device:TPU:80 before, /device:TPU:3 now
where the time goes in v2:
time: 199 us; the launch traced here: 198 us
  Pallas kernels  198 us (99%)
    pallas_call x1, Pallas kernels, on_device(): pl.pallas_call(kernel, out_shape=jax.ShapeDtypeStruct((2, 4, 8, 4, ROWS,...  193 us
    pallas_call x1, Pallas kernels, on_device(): pl.pallas_call(vertical_kernel, out_shape=whole, in_specs=[hbm, pl.BlockS...  5.15 us

profile of v2, /device:TPU:3, one launch (start us, length us, event | category | flops | bytes accessed | tf_op | source)
XLA Modules:
  0.0 198.5 jit_solution(661569554406610552)
XLA Ops:
  0.0 193.3 %shard_map.91 = f32[2,4,8,4,8,512]{5,4,3,2,1,0:T(8,128)} custom-call(f32[2,128,8,512]{3,2,1,0:T(8,128)} %inc_hbm.1, f32[2,128,8,512]{3,2,1,0:T(8,128)} %cx_hbm.1, f32[2,128,8,512]{3,2,1,0:T(8,128)} %cy_hbm.1, f32[256,512]{1,0:T(8,128)} %spec_hbm.1, bf16[2,256,256]{2,1,0:T(8,128)(2,1)} %constant.8.clone.rt_hbm, bf16[2,256,256]{2,1,0:T(8,128)(2,1)} %constant.9.clone.rtt_hbm, ...), custom_call_target="tpu_custom_call" | custom-call | tf_op jit(solution)/shard_map/pallas_call | solution.py:320
  193.3 5.2 %shard_map.92 = f32[2,128,8,512]{3,2,1,0:T(8,128)} custom-call(f32[2,128,8,512]{3,2,1,0:T(8,128)} %bitcast.1, f32[128,128]{1,0:T(8,128)} %v_ref.1), custom_call_target="tpu_custom_call" | custom-call | tf_op jit(solution)/shard_map/pallas_call | solution.py:344

commit v3 on v2

--- a/solution.py
+++ b/solution.py
@@ -176,10 +176,10 @@
         return remote(planes.at[k, pl.ds(0, 6)], planes.at[k, pl.ds(0, 6)], b_send.at[k], b_recv.at[k], {"brick": up})
 
     def c_all(k):
-        return remote(mid_back.at[k, pl.ds(0, 7)], mid_back.at[k, pl.ds(0, 7)], c_send.at[k], c_recv.at[k], {"brick": up})
+        return remote(mid_back.at[k, pl.ds(0, 6)], mid_back.at[k, pl.ds(0, 6)], c_send.at[k], c_recv.at[k], {"brick": up})
 
     def d_all(k):
-        return remote(done.at[k, pl.ds(0, 6)], done.at[k, pl.ds(0, 6)], d_send.at[k], d_recv.at[k], {"brick": up})
+        return remote(done.at[k, pl.ds(0, 28)], done.at[k, pl.ds(0, 28)], d_send.at[k], d_recv.at[k], {"brick": up})
 
     def second_hop(k):
         a_all(k).wait_recv()
@@ -197,20 +197,22 @@
         value = product(split(value), (ct[0], ct[1]))
         value = product((rtt[0], rtt[1]), split(value))
         planes[k] = value.reshape(8, 4, ROWS, COLS)
+        for dy in (1, 3, 2):
+            there, device = y_peer(dy)
+            remote(planes.at[k, :, there], mid_back.at[k, :, y], c_send.at[k], c_recv.at[k], device).start()
+        mid_back[k, :, y] = planes[k, :, y]
+
+    def fourth_hop(k):
+        c_all(k).wait_recv()
         for dx, dz in XZ_ORDER:
             there, device = xz_peer(dx, dz)
-            remote(planes.at[k, there], mid_back.at[k, mine], c_send.at[k], c_recv.at[k], device).start()
-        mid_back[k, mine] = planes[k, mine]
-
-    def fourth_hop(k):
-        c_all(k).wait_recv()
-        for dy in (1, 3, 2):
-            there, device = y_peer(dy)
-            remote(mid_back.at[k, :, there], done.at[k, :, y], d_send.at[k], d_recv.at[k], device).start()
-        done[k, :, y] = mid_back[k, :, y]
+            remote(mid_back.at[k, there], done.at[k, pl.ds(mine * 4, 4)], d_send.at[k], d_recv.at[k], device).start()
+        done[k, pl.ds(mine * 4, 4)] = mid_back[k, mine]
 
     def out_copy(k):
-        return pltpu.make_async_copy(done.at[k], out_hbm.at[1 - lax.rem(k, 2), k // 2], out_sem.at[k])
+        return pltpu.make_async_copy(
+            done.at[k], out_hbm.at[1 - lax.rem(k, 2), pl.ds((k // 2) * CHUNK, CHUNK)], out_sem.at[k]
+        )
 
     def finish(k):
         d_all(k).wait_recv()
@@ -319,7 +321,7 @@
     whole = jax.ShapeDtypeStruct((2, LEVELS, ROWS, COLS), F32)
     horizontal = pl.pallas_call(
         kernel,
-        out_shape=jax.ShapeDtypeStruct((2, 4, 8, 4, ROWS, COLS), F32),
+        out_shape=whole,
         in_specs=[hbm] * 8,
         out_specs=hbm,
         scratch_shapes=[
@@ -327,7 +329,8 @@
             pltpu.VMEM((2, STEPS, 2, LEVELS, COLS), F32),
             pltpu.VMEM((ROWS, LEVELS, COLS), F32),
             pltpu.VMEM((CHUNKS, 32, ROWS, COLS), F32),
-            *[pltpu.VMEM((CHUNKS, 8, 4, ROWS, COLS), F32) for _ in range(4)],
+            *[pltpu.VMEM((CHUNKS, 8, 4, ROWS, COLS), F32) for _ in range(3)],
+            pltpu.VMEM((CHUNKS, 32, ROWS, COLS), F32),
             pltpu.VMEM((NX, COLS), F32),
             *[pltpu.VMEM((2, NX, NX), BF16) for _ in range(2)],
             *[pltpu.VMEM((2, COLS, COLS), BF16) for _ in range(2)],
@@ -348,7 +351,7 @@
         out_specs=hbm,
         scratch_shapes=[pltpu.VMEM(slabs, F32)] * 2 + [dma((2, ROWS))] * 2,
         compiler_params=pltpu.CompilerParams(vmem_limit_bytes=67_043_328),
-    )(horizontal.reshape(whole.shape), vertical)
+    )(horizontal, vertical)
 
 
 def solution(mesh):

time: 199 us -> 185 us (0.930)
  Pallas kernels: 198 us -> 184 us
    pallas_call x1, Pallas kernels: 193 us -> 179 us  [on_device(): pl.pallas_call(kernel, out_shape=whole, in_specs=[hbm] * 8, out_specs=hbm...]
where the time goes in v3:
time: 185 us; the launch traced here: 184 us
  Pallas kernels  184 us (99%)
    pallas_call x1, Pallas kernels, on_device(): pl.pallas_call(kernel, out_shape=whole, in_specs=[hbm] * 8, out_specs=hbm...  179 us
    pallas_call x1, Pallas kernels, on_device(): pl.pallas_call(vertical_kernel, out_shape=whole, in_specs=[hbm, pl.BlockS...  5.15 us

profile of v3, /device:TPU:3, one launch (start us, length us, event | category | flops | bytes accessed | tf_op | source)
XLA Modules:
  0.0 183.9 jit_solution(126373255607128699)
XLA Ops:
  0.0 178.7 %shard_map.91.h_hbm = f32[2,128,8,512]{3,2,1,0:T(8,128)} custom-call(f32[2,128,8,512]{3,2,1,0:T(8,128)} %inc_hbm.1, f32[2,128,8,512]{3,2,1,0:T(8,128)} %cx_hbm.1, f32[2,128,8,512]{3,2,1,0:T(8,128)} %cy_hbm.1, f32[256,512]{1,0:T(8,128)} %spec_hbm.1, bf16[2,256,256]{2,1,0:T(8,128)(2,1)} %constant.8.clone.rt_hbm, bf16[2,256,256]{2,1,0:T(8,128)(2,1)} %constant.9.clone.rtt_hbm, ...), custom_call_target="tpu_custom_call" | custom-call | tf_op jit(solution)/shard_map/pallas_call | solution.py:322
  178.7 5.2 %shard_map.92 = f32[2,128,8,512]{3,2,1,0:T(8,128)} custom-call(f32[2,128,8,512]{3,2,1,0:T(8,128)} %shard_map.91.h_hbm, f32[128,128]{1,0:T(8,128)} %v_ref.1), custom_call_target="tpu_custom_call" | custom-call | tf_op jit(solution)/shard_map/pallas_call | solution.py:347

commit v4 on v3

--- a/solution.py
+++ b/solution.py
@@ -235,10 +235,12 @@
     def _():
         prior[...] = jnp.zeros(prior.shape, F32)
 
-    for copy in loads[4:]:
+    for copy in loads[4:26]:
         copy.wait()
-    for copy in tables:
-        copy.wait()
+
+    def wait_all(copies):
+        for copy in copies:
+            copy.wait()
 
     def each_round(j, carry):
         def within(i):
@@ -255,6 +257,8 @@
             start_chunk(k, 0, prior)
 
         even, odd = lax.rem(j, 2) == 0, lax.rem(j, 2) == 1
+        pl.when(j == 1)(lambda: wait_all(loads[26:]))
+        pl.when(j == 6)(lambda: wait_all(tables))
         for step in range(STEPS, 0, -1):
             stage(j - step + 1, lambda i, step=step: edge_event(i, step))
         stage(j + 3, ahead)

time: 185 us -> 187 us (1.011)
  Pallas kernels: 184 us -> 186 us
    pallas_call x1, Pallas kernels: 179 us -> 181 us  [on_device(): pl.pallas_call(kernel, out_shape=whole, in_specs=[hbm] * 8, out_specs=hbm...]
where the time goes in v4:
time: 187 us; the launch traced here: 186 us
  Pallas kernels  186 us (99%)
    pallas_call x1, Pallas kernels, on_device(): pl.pallas_call(kernel, out_shape=whole, in_specs=[hbm] * 8, out_specs=hbm...  181 us
    pallas_call x1, Pallas kernels, on_device(): pl.pallas_call(vertical_kernel, out_shape=whole, in_specs=[hbm, pl.BlockS...  5.15 us

profile of v4, /device:TPU:3, one launch (start us, length us, event | category | flops | bytes accessed | tf_op | source)
XLA Modules:
  0.0 186.4 jit_solution(17756236932386152460)
XLA Ops:
  0.0 181.2 %shard_map.91.h_hbm = f32[2,128,8,512]{3,2,1,0:T(8,128)} custom-call(f32[2,128,8,512]{3,2,1,0:T(8,128)} %inc_hbm.1, f32[2,128,8,512]{3,2,1,0:T(8,128)} %cx_hbm.1, f32[2,128,8,512]{3,2,1,0:T(8,128)} %cy_hbm.1, f32[256,512]{1,0:T(8,128)} %spec_hbm.1, bf16[2,256,256]{2,1,0:T(8,128)(2,1)} %constant.8.clone.rt_hbm, bf16[2,256,256]{2,1,0:T(8,128)(2,1)} %constant.9.clone.rtt_hbm, ...), custom_call_target="tpu_custom_call" | custom-call | tf_op jit(solution)/shard_map/pallas_call | solution.py:326
  181.2 5.2 %shard_map.92 = f32[2,128,8,512]{3,2,1,0:T(8,128)} custom-call(f32[2,128,8,512]{3,2,1,0:T(8,128)} %shard_map.91.h_hbm, f32[128,128]{1,0:T(8,128)} %v_ref.1), custom_call_target="tpu_custom_call" | custom-call | tf_op jit(solution)/shard_map/pallas_call | solution.py:351
